TPU v7x, 32 devices: a whole 2x2x4 slice. The times are simulated.
32 devices in a mesh: node: 4 (over y, core), rep: 8 (over z, x).
Axes of the slice: x: 2, y: 2, z: 4, core: 2. Of those that a mesh axis runs over, the one named last changes fastest.
Arguments:
- tokens: bfloat16 [8192, 2048], P(('node', 'rep')), may hold values from -60 to 60
- cotangent: bfloat16 [8192, 512], P(('node', 'rep')), may hold values from -6 to 6
- value_weight: bfloat16 [2048, 512], P('node'), may hold values from -0.25 to 0.25
Outputs:
- input_grad: bfloat16 [8192, 2048], P(('node', 'rep'))
- update: float32 [2048, 512], P('node')
All inputs are finite; a program needn't handle non-finite values.
Results may differ from a plain program's by a relative error of at most 0.025.
Values may be sent and summed in bfloat16 or wider, within the bound.
A program may use at most 64 MiB of HBM per device.

v0:
```python
import math
import jax
import jax.numpy as jnp
from jax import lax
from jax.sharding import PartitionSpec as P

DIN = 2048
HD = 128
NS_ITERS = 5
coef_a = 3.4445
coef_b = -4.775
coef_c = 2.0315
epsilon = 1e-07


def per_device(tokens, cotangent, value_weight):
    width = value_weight.shape[1]
    local_rows = value_weight.shape[0]
    heads = width // HD
    input_grad = lax.dot_general(
        cotangent,
        lax.all_gather(value_weight, "node", axis=0, tiled=True),
        (((1,), (1,)), ((), ())),
        preferred_element_type=jnp.float32,
    ).astype(jnp.bfloat16)
    partial_rows = lax.psum_scatter(
        lax.dot_general(
            tokens, cotangent, (((0,), (0,)), ((), ())), preferred_element_type=jnp.float32
        ).astype(jnp.bfloat16),
        "node",
        scatter_dimension=0,
        tiled=True,
    ).astype(jnp.float32)
    gradient = lax.psum(partial_rows, "rep")
    blocks = gradient.reshape(local_rows, heads, HD)
    local_raw = jnp.einsum("rhi,rhj->hij", blocks, blocks, precision=lax.Precision.HIGHEST)
    gram_raw = lax.psum(local_raw, "node")
    squares = jnp.einsum("hii->h", gram_raw)
    divisor = jnp.sqrt(squares) + epsilon
    start_iterate = blocks / divisor[None, :, None]
    gram = gram_raw / (divisor * divisor)[:, None, None]
    identity = jnp.broadcast_to(jnp.eye(HD, dtype=jnp.float32), (heads, HD, HD))
    total = identity
    for step in range(NS_ITERS):
        factor = (
            coef_a * identity
            + coef_b * gram
            + coef_c * jnp.einsum("hij,hjk->hik", gram, gram, precision=lax.Precision.HIGHEST)
        )
        total = jnp.einsum("hij,hjk->hik", total, factor, precision=lax.Precision.HIGHEST)
        if step + 1 < NS_ITERS:
            halfway = jnp.einsum("hij,hjk->hik", gram, factor, precision=lax.Precision.HIGHEST)
            gram = jnp.einsum("hji,hjk->hik", factor, halfway, precision=lax.Precision.HIGHEST)
    iterate = jnp.einsum("rhi,hij->rhj", start_iterate, total, precision=lax.Precision.HIGHEST)
    update = 0.2 * math.sqrt(DIN) * iterate.reshape(local_rows, width)
    return (input_grad, update)


def solution(mesh):
    in_specs = (P(("node", "rep"), None), P(("node", "rep"), None), P("node", None))
    out_specs = (P(("node", "rep"), None), P("node", None))
    return jax.shard_map(
        per_device, mesh=mesh, in_specs=in_specs, out_specs=out_specs, check_vma=False
    )
```

profile of v0, /device:TPU:0, one launch (start us, length us, event | category | flops | bytes accessed | tf_op | source)
XLA Modules:
  0.0 206.4 jit_solution(13655678280055105823)
XLA Ops:
  7.2 0.0 copy-start
  7.2 0.0 reduce-scatter.2.cloned.1.call-start
  7.2 1.2 copy-done
  8.4 3.0 %convolution_convert_fusion = bf16[2048,512]{1,0:T(8,128)(2,1)} fusion(bf16[256,2048]{1,0:T(8,128)(2,1)S(1)} %copy-done, bf16[256,512]{1,0:T(8,128)(2,1)} %param.4), kind=kOutput, calls=%fused_computation | convolution fusion | flops 537919488 | bytes 3407872 | tf_op jit(solution)/shard_map/dot_general | solution.py:27
  11.4 0.0 reduce-scatter.2.cloned.1.call-update
  11.5 0.0 all-reduce.3.cloned.1.call-start
  11.5 34.0 %reduce-scatter.2.cloned.1.call-done = bf16[512,512]{1,0:T(8,128)(2,1)} async-done(((bf16[2048,512]{1,0:T(8,128)(2,1)}), bf16[512,512]{1,0:T(8,128)(2,1)}) %reduce-scatter.2.cloned.1.call-update) | async-done | bytes 524304 | tf_op jit(solution)/shard_map/reduce_scatter | solution.py:26
  45.5 2.1 %copy_bitcast_fusion = f32[512,4,128]{2,0,1:T(8,128)} fusion(bf16[512,512]{1,0:T(8,128)(2,1)} %reduce-scatter.2.cloned.1.call-done), kind=kLoop, calls=%fused_computation.13 | loop fusion | flops 262144 | bytes 1572864 | tf_op jit(solution)/shard_map/reshape | solution.py:35
  47.6 0.0 copy-start.2
  47.6 0.0 all-reduce.3.cloned.1.call-update
  47.6 0.0 all-gather.2.cloned.1.call-start
  47.7 0.7 all-gather.2.cloned.1.call-update
  48.4 0.0 all-reduce.5.cloned.1.call-start
  48.5 79.5 %all-reduce.3.cloned.1.call-done = f32[512,4,128]{2,0,1:T(8,128)} async-done(((f32[512,4,128]{2,0,1:T(8,128)}), f32[512,4,128]{2,0,1:T(8,128)}) %all-reduce.3.cloned.1.call-update) | async-done | bytes 1048592 | tf_op jit(solution)/shard_map/psum | solution.py:34
  128.0 4.1 %fusion.13 = f32[4,128,128]{2,1,0:T(8,128)} fusion(f32[512,4,128]{2,0,1:T(8,128)} %all-reduce.3.cloned.1.call-done), kind=kOutput, calls=%fused_computation.28 | convolution fusion | flops 402653184 | bytes 1310720 | tf_op jit(solution)/shard_map/rhi,rhj->hij/dot_general | solution.py:36
  132.1 0.0 all-reduce.5.cloned.1.call-update
  132.1 19.6 %all-gather.2.cloned.1.call-done = bf16[2048,512]{1,0:T(8,128)(2,1)} async-done(((bf16[512,512]{1,0:T(8,128)(2,1)}), bf16[2048,512]{1,0:T(8,128)(2,1)}) %all-gather.2.cloned.1.call-update) | async-done | bytes 2097168 | tf_op jit(solution)/shard_map/all_gather | solution.py:22
  151.8 0.0 copy-done.2
  151.8 3.3 %convolution_convert_fusion.1 = bf16[256,2048]{1,0:T(8,128)(2,1)} fusion(bf16[256,512]{1,0:T(8,128)(2,1)S(1)} %copy-done.2, bf16[2048,512]{1,0:T(8,128)(2,1)} %all-gather.2.cloned.1.call-done), kind=kOutput, calls=%fused_computation.1 | convolution fusion | flops 537395200 | bytes 3407872 | tf_op jit(solution)/shard_map/dot_general | solution.py:20
  155.1 31.8 %all-reduce.5.cloned.1.call-done = f32[4,128,128]{2,1,0:T(8,128)} async-done(((f32[4,128,128]{2,1,0:T(8,128)}), f32[4,128,128]{2,1,0:T(8,128)}) %all-reduce.5.cloned.1.call-update) | async-done | bytes 262160 | tf_op jit(solution)/shard_map/psum | solution.py:37
  186.8 0.0 copy-start.3
  186.8 1.2 select_reduce_fusion
  188.0 1.6 fusion.4
  189.6 0.4 fusion.7
  190.0 0.0 copy-done.3
  190.0 0.4 fusion.11
  190.5 0.6 fusion.14
  191.1 0.4 fusion.3
  191.4 0.4 fusion.16
  191.8 0.4 fusion.15
  192.2 0.6 fusion.17
  192.9 0.4 fusion.2
  193.2 0.4 fusion.19
  193.6 0.4 fusion.18
  194.0 0.6 fusion.20
  194.7 0.4 fusion.1
  195.0 0.0 copy-start.1
  195.0 0.4 fusion.22
  195.4 0.4 fusion.21
  195.9 0.6 fusion.23
  196.5 0.4 fusion
  196.8 0.6 fusion.24
  197.4 0.0 copy-done.1
  197.5 1.1 convolution_multiply_fusion
  198.5 1.3 copy.11
  (4 shorter events, 0.0 us)
Async XLA Ops:
  7.2 1.2 copy-start
  7.2 38.4 %reduce-scatter.2.cloned.1.call-start = ((), (), s32[]{:S(2)}) async-start(), calls=%async_computation.2 | async-start | bytes 2621440 | tf_op jit(solution)/shard_map/reduce_scatter | solution.py:26
  11.5 116.6 %all-reduce.3.cloned.1.call-start = ((), (), s32[]{:S(2)}) async-start(), calls=%async_computation.3 | async-start | bytes 2097152 | tf_op jit(solution)/shard_map/psum | solution.py:34
  47.6 104.2 %copy-start.2 = (bf16[256,512]{1,0:T(8,128)(2,1)S(1)}, bf16[256,512]{1,0:T(8,128)(2,1)}, u32[]{:S(2)}) copy-start(bf16[256,512]{1,0:T(8,128)(2,1)} %param.4) | copy-start | bytes 786436
  47.6 104.1 %all-gather.2.cloned.1.call-start = ((), (), s32[]{:S(2)}) async-start(), calls=%async_computation.1 | async-start | bytes 2621440 | tf_op jit(solution)/shard_map/all_gather | solution.py:22
  48.4 138.5 %all-reduce.5.cloned.1.call-start = ((), (), s32[]{:S(2)}) async-start(), calls=%async_computation.4 | async-start | bytes 524288 | tf_op jit(solution)/shard_map/psum | solution.py:37
  186.8 3.2 %copy-start.3 = (f32[4,128,128]{2,1,0:T(8,128)S(1)}, f32[4,128,128]{2,1,0:T(8,128)}, u32[]{:S(2)}) copy-start(f32[4,128,128]{2,1,0:T(8,128)} %all-reduce.5.cloned.1.call-done) | copy-start | bytes 786436
  195.0 2.4 %copy-start.1 = (f32[512,4,128]{2,0,1:T(8,128)S(1)}, f32[512,4,128]{2,0,1:T(8,128)}, u32[]{:S(2)}) copy-start(f32[512,4,128]{2,0,1:T(8,128)} %all-reduce.3.cloned.1.call-done) | copy-start | bytes 3145732
Sparse Core Ops, SparseCore 0:
  11.6 33.9 reduce-scatter.1
  49.6 78.3 all-reduce.2
  129.6 22.1 all-gather.1
  154.5 32.2 all-reduce.4
where the time goes:
time: 207 us; the launch traced here: 206 us
  waiting for transfers between devices  166 us (80%)
  matrix products  20.8 us (10%)
  between operations  14 us (7%)
  other arithmetic  3.28 us (2%)
  local copies, waits for them, and re-layouts  2.5 us (1%)
    psum x1, waiting for transfers between devices, per_device(): gradient = lax.psum(partial_rows, 'rep')  79.5 us
    reduce_scatter x1, waiting for transfers between devices, per_device(): lax.psum_scatter(lax.dot_general(tokens, cotangent, (((0,), (0,)), ((), (...  34 us
    psum x1, waiting for transfers between devices, per_device(): gram_raw = lax.psum(local_raw, 'node')  31.8 us
    all_gather x1, waiting for transfers between devices, per_device(): lax.all_gather(value_weight, 'node', axis=0, tiled=True)  19.6 us
  transfers between devices with their start and end apart: 4, of which 4 were waited for; matrix products, arithmetic and copies ran while one was open for 4% of the time, Pallas kernels for 0%

commit v1 on v0

--- a/solution.py
+++ b/solution.py
@@ -34,7 +34,7 @@
     gradient = lax.psum(partial_rows, "rep")
     blocks = gradient.reshape(local_rows, heads, HD)
     local_raw = jnp.einsum("rhi,rhj->hij", blocks, blocks, precision=lax.Precision.HIGHEST)
-    gram_raw = lax.psum(local_raw, "node")
+    gram_raw = jnp.sum(jax.lax.all_gather(local_raw, "node"), 0)
     squares = jnp.einsum("hii->h", gram_raw)
     divisor = jnp.sqrt(squares) + epsilon
     start_iterate = blocks / divisor[None, :, None]

time: 207 us -> 190 us (0.918)
  waiting for transfers between devices: 166 us -> 149 us
    psum x1 -> x0, waiting for transfers between devices: 31.8 us -> none  [per_device(): gram_raw = lax.psum(local_raw, 'node')]
    all_gather x0 -> x1, waiting for transfers between devices: none -> 15.4 us  [per_device(): gram_raw = jnp.sum(jax.lax.all_gather(local_raw, 'node'), 0)]
where the time goes in v1:
time: 190 us; the launch traced here: 189 us
  waiting for transfers between devices  149 us (78%)
  matrix products  19.7 us (10%)
  between operations  14 us (7%)
  other arithmetic  3.56 us (2%)
  local copies, waits for them, and re-layouts  2.49 us (1%)
    psum x1, waiting for transfers between devices, per_device(): gradient = lax.psum(partial_rows, 'rep')  79.6 us
    reduce_scatter x1, waiting for transfers between devices, per_device(): lax.psum_scatter(lax.dot_general(tokens, cotangent, (((0,), (0,)), ((), (...  34 us
    all_gather x1, waiting for transfers between devices, per_device(): lax.all_gather(value_weight, 'node', axis=0, tiled=True)  19.6 us
    all_gather x1, waiting for transfers between devices, per_device(): gram_raw = jnp.sum(jax.lax.all_gather(local_raw, 'node'), 0)  15.4 us
    dot_general x1, matrix products, per_device(): jnp.einsum('rhi,rhj->hij', blocks, blocks, precision=lax.Precision.HIGHEST)  4.11 us
  transfers between devices with their start and end apart: 4, of which 4 were waited for; matrix products, arithmetic and copies ran while one was open for 4% of the time, Pallas kernels for 0%

profile of v1, /device:TPU:0, one launch (start us, length us, event | category | flops | bytes accessed | tf_op | source)
XLA Modules:
  0.0 189.2 jit_solution(14752643389635039903)
XLA Ops:
  7.2 0.0 copy-start
  7.2 0.0 reduce-scatter.2.cloned.1.call-start
  7.2 1.2 copy-done
  8.4 3.0 %convolution_convert_fusion = bf16[2048,512]{1,0:T(8,128)(2,1)} fusion(bf16[256,2048]{1,0:T(8,128)(2,1)S(1)} %copy-done, bf16[256,512]{1,0:T(8,128)(2,1)} %param.4), kind=kOutput, calls=%fused_computation | convolution fusion | flops 537919488 | bytes 3407872 | tf_op jit(solution)/shard_map/dot_general | solution.py:27
  11.4 0.0 reduce-scatter.2.cloned.1.call-update
  11.4 0.0 all-reduce.2.cloned.1.call-start
  11.5 34.0 %reduce-scatter.2.cloned.1.call-done = bf16[512,512]{1,0:T(8,128)(2,1)} async-done(((bf16[2048,512]{1,0:T(8,128)(2,1)}), bf16[512,512]{1,0:T(8,128)(2,1)}) %reduce-scatter.2.cloned.1.call-update) | async-done | bytes 524304 | tf_op jit(solution)/shard_map/reduce_scatter | solution.py:26
  45.5 2.1 %copy_bitcast_fusion = f32[512,4,128]{2,0,1:T(8,128)} fusion(bf16[512,512]{1,0:T(8,128)(2,1)} %reduce-scatter.2.cloned.1.call-done), kind=kLoop, calls=%fused_computation.13 | loop fusion | flops 262144 | bytes 1572864 | tf_op jit(solution)/shard_map/reshape | solution.py:35
  47.6 0.0 copy-start.2
  47.6 0.0 all-reduce.2.cloned.1.call-update
  47.6 0.0 all-gather.4.cloned.1.call-start
  47.7 0.7 all-gather.4.cloned.1.call-update
  48.4 0.0 all-gather.6.cloned.1.call-start
  48.4 79.6 %all-reduce.2.cloned.1.call-done = f32[512,4,128]{2,0,1:T(8,128)} async-done(((f32[512,4,128]{2,0,1:T(8,128)}), f32[512,4,128]{2,0,1:T(8,128)}) %all-reduce.2.cloned.1.call-update) | async-done | bytes 1048592 | tf_op jit(solution)/shard_map/psum | solution.py:34
  128.0 4.1 %fusion.13 = f32[4,128,128]{2,1,0:T(8,128)} fusion(f32[512,4,128]{2,0,1:T(8,128)} %all-reduce.2.cloned.1.call-done), kind=kOutput, calls=%fused_computation.28 | convolution fusion | flops 402653184 | bytes 1310720 | tf_op jit(solution)/shard_map/rhi,rhj->hij/dot_general | solution.py:36
  132.1 0.0 all-gather.6.cloned.1.call-update
  132.2 19.6 %all-gather.4.cloned.1.call-done = bf16[2048,512]{1,0:T(8,128)(2,1)} async-done(((bf16[512,512]{1,0:T(8,128)(2,1)}), bf16[2048,512]{1,0:T(8,128)(2,1)}) %all-gather.4.cloned.1.call-update) | async-done | bytes 2097168 | tf_op jit(solution)/shard_map/all_gather | solution.py:22
  151.8 0.0 copy-done.2
  151.8 3.3 %convolution_convert_fusion.1 = bf16[256,2048]{1,0:T(8,128)(2,1)} fusion(bf16[256,512]{1,0:T(8,128)(2,1)S(1)} %copy-done.2, bf16[2048,512]{1,0:T(8,128)(2,1)} %all-gather.4.cloned.1.call-done), kind=kOutput, calls=%fused_computation.1 | convolution fusion | flops 537395200 | bytes 3407872 | tf_op jit(solution)/shard_map/dot_general | solution.py:20
  155.1 15.4 %all-gather.6.cloned.1.call-done = f32[16,128,128]{2,1,0:T(8,128)} async-done(((f32[4,128,128]{2,1,0:T(8,128)}), f32[16,128,128]{2,1,0:T(8,128)}) %all-gather.6.cloned.1.call-update) | async-done | bytes 1048592 | tf_op jit(solution)/shard_map/all_gather | solution.py:37
  170.5 1.3 reduce_sum.18
  171.8 0.1 select_reduce_fusion
  171.9 0.5 fusion.4
  172.4 0.4 fusion.11
  172.9 0.4 fusion.7
  173.3 0.6 fusion.14
  173.9 0.4 fusion.3
  174.2 0.4 fusion.16
  174.7 0.4 fusion.15
  175.1 0.6 fusion.17
  175.7 0.4 fusion.2
  176.0 0.4 fusion.19
  176.4 0.4 fusion.18
  176.9 0.6 fusion.20
  177.5 0.4 fusion.1
  177.8 0.0 copy-start.1
  177.9 0.4 fusion.22
  178.3 0.4 fusion.21
  178.7 0.6 fusion.23
  179.3 0.4 fusion
  179.6 0.6 fusion.24
  180.2 0.0 copy-done.1
  180.3 1.1 convolution_multiply_fusion
  181.4 1.3 copy.18
  (4 shorter events, 0.0 us)
Async XLA Ops:
  7.2 1.2 copy-start
  7.2 38.3 %reduce-scatter.2.cloned.1.call-start = ((), (), s32[]{:S(2)}) async-start(), calls=%async_computation.2 | async-start | bytes 2621440 | tf_op jit(solution)/shard_map/reduce_scatter | solution.py:26
  11.4 116.6 %all-reduce.2.cloned.1.call-start = ((), (), s32[]{:S(2)}) async-start(), calls=%async_computation.3 | async-start | bytes 2097152 | tf_op jit(solution)/shard_map/psum | solution.py:34
  47.6 104.2 %copy-start.2 = (bf16[256,512]{1,0:T(8,128)(2,1)S(1)}, bf16[256,512]{1,0:T(8,128)(2,1)}, u32[]{:S(2)}) copy-start(bf16[256,512]{1,0:T(8,128)(2,1)} %param.4) | copy-start | bytes 786436
  47.6 104.1 %all-gather.4.cloned.1.call-start = ((), (), s32[]{:S(2)}) async-start(), calls=%async_computation.1 | async-start | bytes 2621440 | tf_op jit(solution)/shard_map/all_gather | solution.py:22
  48.4 122.1 %all-gather.6.cloned.1.call-start = ((), (), s32[]{:S(2)}) async-start(), calls=%async_computation.4 | async-start | bytes 1310720 | tf_op jit(solution)/shard_map/all_gather | solution.py:37
  177.8 2.4 %copy-start.1 = (f32[512,4,128]{2,0,1:T(8,128)S(1)}, f32[512,4,128]{2,0,1:T(8,128)}, u32[]{:S(2)}) copy-start(f32[512,4,128]{2,0,1:T(8,128)} %all-reduce.2.cloned.1.call-done) | copy-start | bytes 3145732
Sparse Core Ops, SparseCore 0:
  11.6 33.9 reduce-scatter.1
  49.6 78.3 all-reduce.1
  129.6 22.1 all-gather.3
  153.8 16.6 all-gather.5
